TPU v7x, 128 devices: a whole 4x4x4 slice. The times are simulated.
128 devices in a mesh: ops: 32 (over z, y, core), site: 4 (over x).
Axes of the slice: x: 4, y: 4, z: 4, core: 2. Of those that a mesh axis runs over, the one named last changes fastest.
Arguments:
- wavefunction: bfloat16 [2048, 2048], replicated, may hold values from -6 to 6
- left_blocks: bfloat16 [256, 16, 192, 192], P('ops', 'site'), may hold values from -0.4375 to 0.4375
- right_blocks: bfloat16 [256, 16, 192, 192], P('ops', 'site'), may hold values from -0.078125 to 0.078125
- left_sector: int32 [2048], replicated, may hold values from 0 to 15, as said below
- right_sector: int32 [2048], replicated, may hold values from 0 to 15, as said below
- term_count: int32 [32], P('ops'), may hold values from 1 to 8, as said below
- left_energy: float32 [2048], replicated, may hold values from -1 to 1
- right_energy: float32 [2048], replicated, may hold values from -1 to 1
- subspace: bfloat16 [2, 16, 192, 2048], P(None, 'site'), may hold values from -0.0078125 to 0.0078125
Outputs:
- sigma: bfloat16 [16, 192, 2048], P('site')
- projections: float32 [2], replicated
Inputs may be any that keep to these rules, and one draw needn't show every extreme that they name: `left_sector`: sector ids never fall along the bond; each of the 16 sectors has 1 to 192 states and one has exactly 192. `right_sector`: sector ids never fall along the bond; each of the 16 sectors has 1 to 192 states and one has exactly 192. `term_count`: some group has all 8 slots live.
All inputs are finite; a program needn't handle non-finite values.
Results may differ from a plain program's by a relative error of at most 0.0045.
Values may be sent and summed in bfloat16 or wider, within the bound.
No kernel may reach another device: no remote copies, remote signals or barrier semaphores. Data moves between devices by JAX's collectives and lax.ppermute only.
A program may use at most 192 MiB of HBM per device.

v0:
```python
import jax
import jax.numpy as jnp
from jax import lax
from jax.sharding import PartitionSpec as P


def from_everyone(value, axis):
    size = lax.axis_size(axis)
    return lax.all_to_all(
        jnp.broadcast_to(value[None], (size, *value.shape)), axis, 0, 0, tiled=True
    )


def over_copies(value, axis):
    return from_everyone(value, axis).sum(axis=0)


def sector_tables(sector_ids, sectors):
    labels = jnp.arange(sectors, dtype=jnp.int32)
    sector_starts = jnp.sum((sector_ids[None, :] < labels[:, None]).astype(jnp.int32), axis=1)
    sector_sizes = jnp.sum((sector_ids[None, :] == labels[:, None]).astype(jnp.int32), axis=1)
    return (sector_starts, sector_sizes)


def block_mask(size_now, widest):
    inside = jnp.arange(widest, dtype=jnp.int32) < size_now
    return inside[:, None] & inside[None, :]


def correlations(vectors, values):
    return jnp.sum(vectors.astype(jnp.float32) * values[None], axis=(1, 2, 3))


def local(
    wavefunction,
    left_blocks,
    right_blocks,
    left_sector,
    right_sector,
    term_count,
    left_energy,
    right_energy,
    subspace,
):
    slot_count = left_blocks.shape[0]
    sec_dev = left_blocks.shape[1]
    widest = left_blocks.shape[2]
    bond_dim = wavefunction.shape[0]
    row_count = sec_dev * widest
    sectors = sec_dev * lax.axis_size("site")
    left_start, left_size = sector_tables(left_sector, sectors)
    right_start, right_size = sector_tables(right_sector, sectors)
    active = term_count[0]
    first_sector = lax.axis_index("site") * sec_dev
    psi_padded = jnp.concatenate(
        [wavefunction, jnp.zeros((widest, bond_dim), wavefunction.dtype)], axis=0
    )
    energy_padded = jnp.concatenate([left_energy, jnp.zeros((widest,), jnp.float32)])
    psi_slabs = []
    energies = []
    left_masks = []
    inside_rows = []
    for within in range(sec_dev):
        sector = first_sector + within
        row_start = left_start[sector]
        size_now = left_size[sector]
        psi_slabs.append(lax.dynamic_slice_in_dim(psi_padded, row_start, widest, 0))
        energies.append(lax.dynamic_slice_in_dim(energy_padded, row_start, widest, 0))
        inside = jnp.arange(widest, dtype=jnp.int32) < size_now
        inside_rows.append(inside)
        left_masks.append(inside[:, None] & inside[None, :])

    def left_term(term_idx, stacked):
        blocks = lax.dynamic_index_in_dim(left_blocks, term_idx, 0, False)
        pieces = []
        for within in range(sec_dev):
            masked = jnp.where(left_masks[within], blocks[within], jnp.zeros((), blocks.dtype))
            pieces.append(jnp.dot(masked, psi_slabs[within], preferred_element_type=jnp.float32))
        left_image = jnp.concatenate(pieces, axis=0).astype(jnp.bfloat16)
        left_image = jnp.concatenate(
            [left_image, jnp.zeros((row_count, widest), jnp.bfloat16)], axis=1
        )
        return lax.dynamic_update_index_in_dim(stacked, left_image, term_idx, 0)

    images = lax.fori_loop(
        0, active, left_term, jnp.zeros((slot_count, row_count, bond_dim + widest), jnp.bfloat16)
    )
    part_blocks = lax.all_gather(right_blocks, "site", axis=1, tiled=True)

    def one_sector(within, summed):
        col_start = right_start[within]
        keep_mask = block_mask(right_size[within], widest)
        blocks = lax.dynamic_index_in_dim(part_blocks, within, 1, False)

        def add_term(term_idx, running):
            window = lax.dynamic_slice_in_dim(
                lax.dynamic_index_in_dim(images, term_idx, 0, False), col_start, widest, 1
            )
            one_block = jnp.where(
                keep_mask,
                lax.dynamic_index_in_dim(blocks, term_idx, 0, False),
                jnp.zeros((), blocks.dtype),
            )
            return running + lax.dot_general(
                window, one_block, (((1,), (1,)), ((), ())), preferred_element_type=jnp.float32
            )

        added = lax.fori_loop(0, active, add_term, jnp.zeros((row_count, widest), jnp.float32))
        previous = lax.dynamic_slice_in_dim(summed, col_start, widest, 1)
        return lax.dynamic_update_slice_in_dim(summed, previous + added, col_start, 1)

    folded = lax.fori_loop(
        0, part_blocks.shape[1], one_sector, jnp.zeros((row_count, bond_dim + widest), jnp.float32)
    )
    partial_value = folded[:, :bond_dim].reshape(sec_dev, widest, bond_dim)
    psi_mine = jnp.where(
        jnp.stack(inside_rows)[:, :, None],
        jnp.stack(psi_slabs).astype(jnp.float32),
        jnp.float32(0.0),
    )
    energy_mine = jnp.stack(energies)
    diagonal = (energy_mine[:, :, None] + right_energy[None, None, :]) * psi_mine
    sigma_full = lax.psum(partial_value, "ops") + diagonal
    sigma_out = sigma_full.astype(jnp.bfloat16)
    projections = over_copies(correlations(subspace, sigma_full), "site")
    return (sigma_out, projections)


def solution(mesh):
    in_specs = (
        P(),
        P("ops", "site", None, None),
        P("ops", "site", None, None),
        P(),
        P(),
        P("ops"),
        P(),
        P(),
        P(None, "site", None, None),
    )
    out_specs = (P("site", None, None), P())
    return jax.shard_map(local, mesh=mesh, in_specs=in_specs, out_specs=out_specs, check_vma=False)
```

profile of v0, /device:TPU:24, one launch (start us, length us, event | category | flops | bytes accessed | tf_op | source)
XLA Modules:
  0.0 715.6 jit_solution(18417771134688194427)
XLA Ops:
  7.2 3.9 copy.17
  22.2 5.3 pad_dynamic-slice_fusion
  27.5 9.9 %broadcast_in_dim.39 = bf16[8,768,2240]{2,1,0:T(8,128)(2,1)} broadcast(bf16[]{:T(256)} %constant.184.clone.1), dimensions={} | broadcast | bytes 27525122 | tf_op jit(solution)/shard_map/broadcast_in_dim | solution.py:86
  37.4 40.1 %while.63 = (s32[]{:T(128)}, bf16[8,768,2240]{2,1,0:T(8,128)(2,1)}, s32[]{:T(128)}, bf16[8,4,192,192]{3,2,1,0:T(8,128)(2,1)}, bf16[192,2048]{1,0:T(8,128)(2,1)},...) while((s32[]{:T(128)}, bf16[8,768,2240]{2,1,0:T(8,128)(2,1)}, ...), condition=%wide.region_5.6_spmd.clone, body=%wide.region_4.5_spmd.clone.sunk | while | flops 628211712 | bytes 13373707 | solution.py:85
  53.7 3.3 fusion.67
  63.5 3.4 fusion.67
  73.4 3.4 fusion.67
  77.5 54.4 %all-gather.2.cloned.1.call-done = bf16[8,16,192,192]{3,2,0,1:T(8,128)(2,1)} async-done(((bf16[8,4,192,192]{3,2,0,1:T(8,128)(2,1)}), bf16[8,16,192,192]{3,2,0,1:T(8,128)(2,1)}) %all-gather.2.cloned.1.call-update) | async-done | bytes 9437200 | tf_op jit(solution)/shard_map/all_gather | solution.py:88
  131.9 3.3 broadcast_in_dim.38
  135.2 292.4 %while.62 = (s32[]{:T(128)}, f32[768,2240]{0,1:T(8,128)}, s32[16]{0:T(128)S(1)}, bf16[8,16,192,192]{3,2,0,1:T(8,128)(2,1)}, s32[16]{0:T(128)S(1)}, /*index=5*/s3...) while((s32[]{:T(128)}, f32[768,2240]{0,1:T(8,128)}, ...), condition=%wide.region_9.10_spmd, body=%wide.region_6.9_spmd.sunk | while | flops 56991944 | bytes 6391994 | solution.py:112
  140.3 9.1 %while.64 = (s32[]{:T(128)}, f32[768,192]{0,1:T(8,128)S(1)}, s32[]{:T(128)}, bf16[8,768,2240]{2,1,0:T(8,128)(2,1)}, s32[]{:T(128)}, /*index=5*/bf16[8,192,192]{2...) while((s32[]{:T(128)}, f32[768,192]{0,1:T(8,128)S(1)}, ...), condition=%wide.region_8.8_spmd.clone, body=%wide.region_7.7_spmd.clone.sunk | while | flops 56844292 | bytes 1672871 | solution.py:108
  158.5 9.1 %while.64 = (s32[]{:T(128)}, f32[768,192]{0,1:T(8,128)S(1)}, s32[]{:T(128)}, bf16[8,768,2240]{2,1,0:T(8,128)(2,1)}, s32[]{:T(128)}, /*index=5*/bf16[8,192,192]{2...) while((s32[]{:T(128)}, f32[768,192]{0,1:T(8,128)S(1)}, ...), condition=%wide.region_8.8_spmd.clone, body=%wide.region_7.7_spmd.clone.sunk | while | flops 56844292 | bytes 1672871 | solution.py:108
  176.8 9.1 %while.64 = (s32[]{:T(128)}, f32[768,192]{0,1:T(8,128)S(1)}, s32[]{:T(128)}, bf16[8,768,2240]{2,1,0:T(8,128)(2,1)}, s32[]{:T(128)}, /*index=5*/bf16[8,192,192]{2...) while((s32[]{:T(128)}, f32[768,192]{0,1:T(8,128)S(1)}, ...), condition=%wide.region_8.8_spmd.clone, body=%wide.region_7.7_spmd.clone.sunk | while | flops 56844292 | bytes 1672871 | solution.py:108
  195.1 9.1 %while.64 = (s32[]{:T(128)}, f32[768,192]{0,1:T(8,128)S(1)}, s32[]{:T(128)}, bf16[8,768,2240]{2,1,0:T(8,128)(2,1)}, s32[]{:T(128)}, /*index=5*/bf16[8,192,192]{2...) while((s32[]{:T(128)}, f32[768,192]{0,1:T(8,128)S(1)}, ...), condition=%wide.region_8.8_spmd.clone, body=%wide.region_7.7_spmd.clone.sunk | while | flops 56844292 | bytes 1672871 | solution.py:108
  213.4 9.1 %while.64 = (s32[]{:T(128)}, f32[768,192]{0,1:T(8,128)S(1)}, s32[]{:T(128)}, bf16[8,768,2240]{2,1,0:T(8,128)(2,1)}, s32[]{:T(128)}, /*index=5*/bf16[8,192,192]{2...) while((s32[]{:T(128)}, f32[768,192]{0,1:T(8,128)S(1)}, ...), condition=%wide.region_8.8_spmd.clone, body=%wide.region_7.7_spmd.clone.sunk | while | flops 56844292 | bytes 1672871 | solution.py:108
  231.6 9.1 %while.64 = (s32[]{:T(128)}, f32[768,192]{0,1:T(8,128)S(1)}, s32[]{:T(128)}, bf16[8,768,2240]{2,1,0:T(8,128)(2,1)}, s32[]{:T(128)}, /*index=5*/bf16[8,192,192]{2...) while((s32[]{:T(128)}, f32[768,192]{0,1:T(8,128)S(1)}, ...), condition=%wide.region_8.8_spmd.clone, body=%wide.region_7.7_spmd.clone.sunk | while | flops 56844292 | bytes 1672871 | solution.py:108
  249.9 9.1 %while.64 = (s32[]{:T(128)}, f32[768,192]{0,1:T(8,128)S(1)}, s32[]{:T(128)}, bf16[8,768,2240]{2,1,0:T(8,128)(2,1)}, s32[]{:T(128)}, /*index=5*/bf16[8,192,192]{2...) while((s32[]{:T(128)}, f32[768,192]{0,1:T(8,128)S(1)}, ...), condition=%wide.region_8.8_spmd.clone, body=%wide.region_7.7_spmd.clone.sunk | while | flops 56844292 | bytes 1672871 | solution.py:108
  268.2 9.1 %while.64 = (s32[]{:T(128)}, f32[768,192]{0,1:T(8,128)S(1)}, s32[]{:T(128)}, bf16[8,768,2240]{2,1,0:T(8,128)(2,1)}, s32[]{:T(128)}, /*index=5*/bf16[8,192,192]{2...) while((s32[]{:T(128)}, f32[768,192]{0,1:T(8,128)S(1)}, ...), condition=%wide.region_8.8_spmd.clone, body=%wide.region_7.7_spmd.clone.sunk | while | flops 56844292 | bytes 1672871 | solution.py:108
  286.5 9.1 %while.64 = (s32[]{:T(128)}, f32[768,192]{0,1:T(8,128)S(1)}, s32[]{:T(128)}, bf16[8,768,2240]{2,1,0:T(8,128)(2,1)}, s32[]{:T(128)}, /*index=5*/bf16[8,192,192]{2...) while((s32[]{:T(128)}, f32[768,192]{0,1:T(8,128)S(1)}, ...), condition=%wide.region_8.8_spmd.clone, body=%wide.region_7.7_spmd.clone.sunk | while | flops 56844292 | bytes 1672871 | solution.py:108
  304.7 9.1 %while.64 = (s32[]{:T(128)}, f32[768,192]{0,1:T(8,128)S(1)}, s32[]{:T(128)}, bf16[8,768,2240]{2,1,0:T(8,128)(2,1)}, s32[]{:T(128)}, /*index=5*/bf16[8,192,192]{2...) while((s32[]{:T(128)}, f32[768,192]{0,1:T(8,128)S(1)}, ...), condition=%wide.region_8.8_spmd.clone, body=%wide.region_7.7_spmd.clone.sunk | while | flops 56844292 | bytes 1672871 | solution.py:108
  323.0 9.1 %while.64 = (s32[]{:T(128)}, f32[768,192]{0,1:T(8,128)S(1)}, s32[]{:T(128)}, bf16[8,768,2240]{2,1,0:T(8,128)(2,1)}, s32[]{:T(128)}, /*index=5*/bf16[8,192,192]{2...) while((s32[]{:T(128)}, f32[768,192]{0,1:T(8,128)S(1)}, ...), condition=%wide.region_8.8_spmd.clone, body=%wide.region_7.7_spmd.clone.sunk | while | flops 56844292 | bytes 1672871 | solution.py:108
  341.3 9.1 %while.64 = (s32[]{:T(128)}, f32[768,192]{0,1:T(8,128)S(1)}, s32[]{:T(128)}, bf16[8,768,2240]{2,1,0:T(8,128)(2,1)}, s32[]{:T(128)}, /*index=5*/bf16[8,192,192]{2...) while((s32[]{:T(128)}, f32[768,192]{0,1:T(8,128)S(1)}, ...), condition=%wide.region_8.8_spmd.clone, body=%wide.region_7.7_spmd.clone.sunk | while | flops 56844292 | bytes 1672871 | solution.py:108
  359.6 9.1 %while.64 = (s32[]{:T(128)}, f32[768,192]{0,1:T(8,128)S(1)}, s32[]{:T(128)}, bf16[8,768,2240]{2,1,0:T(8,128)(2,1)}, s32[]{:T(128)}, /*index=5*/bf16[8,192,192]{2...) while((s32[]{:T(128)}, f32[768,192]{0,1:T(8,128)S(1)}, ...), condition=%wide.region_8.8_spmd.clone, body=%wide.region_7.7_spmd.clone.sunk | while | flops 56844292 | bytes 1672871 | solution.py:108
  377.8 9.1 %while.64 = (s32[]{:T(128)}, f32[768,192]{0,1:T(8,128)S(1)}, s32[]{:T(128)}, bf16[8,768,2240]{2,1,0:T(8,128)(2,1)}, s32[]{:T(128)}, /*index=5*/bf16[8,192,192]{2...) while((s32[]{:T(128)}, f32[768,192]{0,1:T(8,128)S(1)}, ...), condition=%wide.region_8.8_spmd.clone, body=%wide.region_7.7_spmd.clone.sunk | while | flops 56844292 | bytes 1672871 | solution.py:108
  396.1 9.1 %while.64 = (s32[]{:T(128)}, f32[768,192]{0,1:T(8,128)S(1)}, s32[]{:T(128)}, bf16[8,768,2240]{2,1,0:T(8,128)(2,1)}, s32[]{:T(128)}, /*index=5*/bf16[8,192,192]{2...) while((s32[]{:T(128)}, f32[768,192]{0,1:T(8,128)S(1)}, ...), condition=%wide.region_8.8_spmd.clone, body=%wide.region_7.7_spmd.clone.sunk | while | flops 56844292 | bytes 1672871 | solution.py:108
  414.4 9.1 %while.64 = (s32[]{:T(128)}, f32[768,192]{0,1:T(8,128)S(1)}, s32[]{:T(128)}, bf16[8,768,2240]{2,1,0:T(8,128)(2,1)}, s32[]{:T(128)}, /*index=5*/bf16[8,192,192]{2...) while((s32[]{:T(128)}, f32[768,192]{0,1:T(8,128)S(1)}, ...), condition=%wide.region_8.8_spmd.clone, body=%wide.region_7.7_spmd.clone.sunk | while | flops 56844292 | bytes 1672871 | solution.py:108
  427.6 5.8 slice.19
  433.5 6.6 copy.18
  442.9 246.8 %all-reduce.5.cloned.1.call-done = f32[4,192,2048]{2,1,0:T(8,128)} async-done(((f32[4,192,2048]{2,1,0:T(8,128)}), f32[4,192,2048]{2,1,0:T(8,128)}) %all-reduce.5.cloned.1.call-update) | async-done | bytes 6291472 | tf_op jit(solution)/shard_map/psum | solution.py:123
  689.7 4.7 fusion.49
  694.4 4.6 multiply_reduce_fusion
  698.9 9.3 %all_to_all.6 = f32[4,1,2]{2,1,0:T(1,128)S(1)} all-to-all(f32[4,1,2]{2,1,0:T(1,128)S(1)} %broadcast_in_dim.42), channel_id=1, replica_groups=mesh['ops'=32,'site'=4] {'site'}, dimensions={0} | all-to-all | bytes 64 | tf_op jit(solution)/shard_map/all_to_all | solution.py:9
  (225 shorter events, 240.5 us)
Async XLA Ops:
  7.2 4.0 copy-start.4
  7.2 14.8 %copy-start.5 = (s32[2048]{0:T(1024)S(1)}, s32[2048]{0:T(1024)}, u32[]{:S(2)}) copy-start(s32[2048]{0:T(1024)} %param.19) | copy-start | bytes 24580
  7.2 124.7 %all-gather.2.cloned.1.call-start = ((), (), s32[]{:S(2)}) async-start(), calls=%async_computation.1 | async-start | bytes 15728640 | tf_op jit(solution)/shard_map/all_gather | solution.py:88
  11.1 678.5 %all-reduce.5.cloned.1.call-start = ((), (), s32[]{:S(2)}) async-start(), calls=%async_computation.2 | async-start | bytes 12582912 | tf_op jit(solution)/shard_map/psum | solution.py:123
  440.1 2.7 copy-start.3
  440.1 249.5 %copy-start = (bf16[192,2048]{1,0:T(8,128)(2,1)S(1)}, bf16[192,2048]{1,0:T(8,128)(2,1)}, u32[]{:S(2)}) copy-start(bf16[192,2048]{1,0:T(8,128)(2,1)} %get-tuple-element.834) | copy-start | bytes 2359300
  440.1 249.5 %copy-start.1 = (bf16[192,2048]{1,0:T(8,128)(2,1)S(1)}, bf16[192,2048]{1,0:T(8,128)(2,1)}, u32[]{:S(2)}) copy-start(bf16[192,2048]{1,0:T(8,128)(2,1)} %get-tuple-element.835) | copy-start | bytes 2359300
  440.1 249.5 %copy-start.2 = (f32[2048]{0:T(1024)S(1)}, f32[2048]{0:T(1024)}, u32[]{:S(2)}) copy-start(f32[2048]{0:T(1024)} %param.22) | copy-start | bytes 24580
Sparse Core Ops, SparseCore 0:
  11.3 120.6 all-gather.1
  440.3 249.3 all-reduce.4
where the time goes:
time: 727 us; the launch traced here: 716 us
  waiting for transfers between devices  301 us (41%)
  local copies, waits for them, and re-layouts  121 us (17%)
  matrix products  116 us (16%)
  loops' own time  88.7 us (12%)
  other arithmetic  57.3 us (8%)
  between operations  21.6 us (3%)
  blocking collectives  9.32 us (1%)
    psum x1, waiting for transfers between devices, local(): sigma_full = lax.psum(partial_value, 'ops') + diagonal  247 us
    dot_general x64, matrix products, add_term(): lax.dot_general(window, one_block, (((1,), (1,)), ((), ())), preferred_el...  92.6 us
    all_gather x1, waiting for transfers between devices, local(): part_blocks = lax.all_gather(right_blocks, 'site', axis=1, tiled=True)  54.4 us
    another operation x16, loops' own time, one_sector(): lax.fori_loop(0, active, add_term, jnp.zeros((row_count, widest), jnp.flo...  53.6 us
    dynamic_update_slice x16, local copies, waits for them, and re-layouts, one_sector(): lax.dynamic_update_slice_in_dim(summed, previous + added, col_start, 1)  47.3 us
    another operation x1, loops' own time, local(): lax.fori_loop(0, part_blocks.shape[1], one_sector, jnp.zeros((row_count,...  31.6 us
    dot_general x16, matrix products, left_term(): jnp.dot(masked, psi_slabs[within], preferred_element_type=jnp.float32)  23.3 us
    squeeze x16, local copies, waits for them, and re-layouts, one_sector(): blocks = lax.dynamic_index_in_dim(part_blocks, within, 1, False)  19.1 us
  transfers between devices with their start and end apart: 2, of which 2 were waited for; matrix products, arithmetic and copies ran while one was open for 8% of the time, Pallas kernels for 0%

commit v1 on v0

--- a/solution.py
+++ b/solution.py
@@ -85,7 +85,9 @@
     images = lax.fori_loop(
         0, active, left_term, jnp.zeros((slot_count, row_count, bond_dim + widest), jnp.bfloat16)
     )
-    part_blocks = lax.all_gather(right_blocks, "site", axis=1, tiled=True)
+    part_blocks = jnp.concatenate(
+        lax.all_to_all(jnp.stack([right_blocks] * lax.axis_size("site")), "site", 0, 0), axis=1
+    )
 
     def one_sector(within, summed):
         col_start = right_start[within]

time: 727 us -> 755 us (1.039)
  waiting for transfers between devices: 301 us -> 319 us
    all_to_all x0 -> x1, waiting for transfers between devices: none -> 73.8 us  [local(): lax.all_to_all(jnp.stack([right_blocks] * lax.axis_size('site')), 'site',...]
    all_gather x1 -> x0, waiting for transfers between devices: 54.4 us -> none  [local(): part_blocks = lax.all_gather(right_blocks, 'site', axis=1, tiled=True)]
where the time goes in v1:
time: 755 us; the launch traced here: 743 us
  waiting for transfers between devices  319 us (42%)
  local copies, waits for them, and re-layouts  126 us (17%)
  matrix products  116 us (15%)
  loops' own time  88 us (12%)
  other arithmetic  56.5 us (7%)
  between operations  21.6 us (3%)
  blocking collectives  9.32 us (1%)
    psum x1, waiting for transfers between devices, local(): sigma_full = lax.psum(partial_value, 'ops') + diagonal  245 us
    dot_general x64, matrix products, add_term(): lax.dot_general(window, one_block, (((1,), (1,)), ((), ())), preferred_el...  92.6 us
    all_to_all x1, waiting for transfers between devices, local(): lax.all_to_all(jnp.stack([right_blocks] * lax.axis_size('site')), 'site',...  73.8 us
    another operation x16, loops' own time, one_sector(): lax.fori_loop(0, active, add_term, jnp.zeros((row_count, widest), jnp.flo...  53.6 us
    dynamic_update_slice x16, local copies, waits for them, and re-layouts, one_sector(): lax.dynamic_update_slice_in_dim(summed, previous + added, col_start, 1)  47.3 us
    another operation x1, loops' own time, local(): lax.fori_loop(0, part_blocks.shape[1], one_sector, jnp.zeros((row_count,...  30.9 us
    dot_general x16, matrix products, left_term(): jnp.dot(masked, psi_slabs[within], preferred_element_type=jnp.float32)  23.2 us
    squeeze x16, local copies, waits for them, and re-layouts, one_sector(): blocks = lax.dynamic_index_in_dim(part_blocks, within, 1, False)  19.1 us
  transfers between devices with their start and end apart: 2, of which 2 were waited for; matrix products, arithmetic and copies ran while one was open for 8% of the time, Pallas kernels for 0%

profile of v1, /device:TPU:24, one launch (start us, length us, event | category | flops | bytes accessed | tf_op | source)
XLA Modules:
  0.0 743.4 jit_solution(13401848723885093831)
XLA Ops:
  9.3 6.2 stack.44
  15.4 6.5 all-to-all-start
  33.0 4.9 pad_dynamic-slice_fusion
  38.0 9.4 %broadcast_in_dim.39 = bf16[8,768,2240]{2,1,0:T(8,128)(2,1)} broadcast(bf16[]{:T(256)} %constant.184.clone.1), dimensions={} | broadcast | bytes 27525122 | tf_op jit(solution)/shard_map/broadcast_in_dim | solution.py:86
  47.4 39.8 %while.63 = (s32[]{:T(128)}, bf16[8,768,2240]{2,1,0:T(8,128)(2,1)}, s32[]{:T(128)}, bf16[8,4,192,192]{3,2,1,0:T(8,128)(2,1)}, bf16[192,2048]{1,0:T(8,128)(2,1)},...) while((s32[]{:T(128)}, bf16[8,768,2240]{2,1,0:T(8,128)(2,1)}, ...), condition=%wide.region_5.6_spmd.clone, body=%wide.region_4.5_spmd.clone.sunk | while | flops 628211712 | bytes 13373707 | solution.py:85
  63.7 3.3 fusion.67
  73.5 3.3 fusion.67
  87.2 73.8 %all-to-all-done = bf16[4,8,4,192,192]{4,3,1,2,0:T(8,128)(2,1)} async-done(((bf16[4,8,4,192,192]{4,3,1,2,0:T(8,128)(2,1)}), bf16[4,8,4,192,192]{4,3,1,2,0:T(8,128)(2,1)}, u32[]{:S(2)}, u32[]{:S(2)}) %all-to-all-start) | async-done | bytes 9437216 | tf_op jit(solution)/shard_map/all_to_all | solution.py:89
  161.0 3.3 broadcast_in_dim.38
  164.3 292.5 %while.62 = (s32[]{:T(128)}, f32[768,2240]{0,1:T(8,128)}, s32[16]{0:T(128)S(1)}, bf16[8,16,192,192]{3,2,0,1:T(8,128)(2,1)}, s32[16]{0:T(128)S(1)}, /*index=5*/s3...) while((s32[]{:T(128)}, f32[768,2240]{0,1:T(8,128)}, ...), condition=%wide.region_9.10_spmd, body=%wide.region_6.9_spmd.sunk | while | flops 56991944 | bytes 6391994 | solution.py:114
  169.4 9.1 %while.64 = (s32[]{:T(128)}, f32[768,192]{0,1:T(8,128)S(1)}, s32[]{:T(128)}, bf16[8,768,2240]{2,1,0:T(8,128)(2,1)}, s32[]{:T(128)}, /*index=5*/bf16[8,192,192]{2...) while((s32[]{:T(128)}, f32[768,192]{0,1:T(8,128)S(1)}, ...), condition=%wide.region_8.8_spmd.clone, body=%wide.region_7.7_spmd.clone.sunk | while | flops 56844292 | bytes 1672871 | solution.py:110
  187.6 9.1 %while.64 = (s32[]{:T(128)}, f32[768,192]{0,1:T(8,128)S(1)}, s32[]{:T(128)}, bf16[8,768,2240]{2,1,0:T(8,128)(2,1)}, s32[]{:T(128)}, /*index=5*/bf16[8,192,192]{2...) while((s32[]{:T(128)}, f32[768,192]{0,1:T(8,128)S(1)}, ...), condition=%wide.region_8.8_spmd.clone, body=%wide.region_7.7_spmd.clone.sunk | while | flops 56844292 | bytes 1672871 | solution.py:110
  205.9 9.1 %while.64 = (s32[]{:T(128)}, f32[768,192]{0,1:T(8,128)S(1)}, s32[]{:T(128)}, bf16[8,768,2240]{2,1,0:T(8,128)(2,1)}, s32[]{:T(128)}, /*index=5*/bf16[8,192,192]{2...) while((s32[]{:T(128)}, f32[768,192]{0,1:T(8,128)S(1)}, ...), condition=%wide.region_8.8_spmd.clone, body=%wide.region_7.7_spmd.clone.sunk | while | flops 56844292 | bytes 1672871 | solution.py:110
  224.2 9.1 %while.64 = (s32[]{:T(128)}, f32[768,192]{0,1:T(8,128)S(1)}, s32[]{:T(128)}, bf16[8,768,2240]{2,1,0:T(8,128)(2,1)}, s32[]{:T(128)}, /*index=5*/bf16[8,192,192]{2...) while((s32[]{:T(128)}, f32[768,192]{0,1:T(8,128)S(1)}, ...), condition=%wide.region_8.8_spmd.clone, body=%wide.region_7.7_spmd.clone.sunk | while | flops 56844292 | bytes 1672871 | solution.py:110
  242.5 9.1 %while.64 = (s32[]{:T(128)}, f32[768,192]{0,1:T(8,128)S(1)}, s32[]{:T(128)}, bf16[8,768,2240]{2,1,0:T(8,128)(2,1)}, s32[]{:T(128)}, /*index=5*/bf16[8,192,192]{2...) while((s32[]{:T(128)}, f32[768,192]{0,1:T(8,128)S(1)}, ...), condition=%wide.region_8.8_spmd.clone, body=%wide.region_7.7_spmd.clone.sunk | while | flops 56844292 | bytes 1672871 | solution.py:110
  260.8 9.1 %while.64 = (s32[]{:T(128)}, f32[768,192]{0,1:T(8,128)S(1)}, s32[]{:T(128)}, bf16[8,768,2240]{2,1,0:T(8,128)(2,1)}, s32[]{:T(128)}, /*index=5*/bf16[8,192,192]{2...) while((s32[]{:T(128)}, f32[768,192]{0,1:T(8,128)S(1)}, ...), condition=%wide.region_8.8_spmd.clone, body=%wide.region_7.7_spmd.clone.sunk | while | flops 56844292 | bytes 1672871 | solution.py:110
  279.1 9.1 %while.64 = (s32[]{:T(128)}, f32[768,192]{0,1:T(8,128)S(1)}, s32[]{:T(128)}, bf16[8,768,2240]{2,1,0:T(8,128)(2,1)}, s32[]{:T(128)}, /*index=5*/bf16[8,192,192]{2...) while((s32[]{:T(128)}, f32[768,192]{0,1:T(8,128)S(1)}, ...), condition=%wide.region_8.8_spmd.clone, body=%wide.region_7.7_spmd.clone.sunk | while | flops 56844292 | bytes 1672871 | solution.py:110
  297.4 9.1 %while.64 = (s32[]{:T(128)}, f32[768,192]{0,1:T(8,128)S(1)}, s32[]{:T(128)}, bf16[8,768,2240]{2,1,0:T(8,128)(2,1)}, s32[]{:T(128)}, /*index=5*/bf16[8,192,192]{2...) while((s32[]{:T(128)}, f32[768,192]{0,1:T(8,128)S(1)}, ...), condition=%wide.region_8.8_spmd.clone, body=%wide.region_7.7_spmd.clone.sunk | while | flops 56844292 | bytes 1672871 | solution.py:110
  315.6 9.1 %while.64 = (s32[]{:T(128)}, f32[768,192]{0,1:T(8,128)S(1)}, s32[]{:T(128)}, bf16[8,768,2240]{2,1,0:T(8,128)(2,1)}, s32[]{:T(128)}, /*index=5*/bf16[8,192,192]{2...) while((s32[]{:T(128)}, f32[768,192]{0,1:T(8,128)S(1)}, ...), condition=%wide.region_8.8_spmd.clone, body=%wide.region_7.7_spmd.clone.sunk | while | flops 56844292 | bytes 1672871 | solution.py:110
  333.9 9.1 %while.64 = (s32[]{:T(128)}, f32[768,192]{0,1:T(8,128)S(1)}, s32[]{:T(128)}, bf16[8,768,2240]{2,1,0:T(8,128)(2,1)}, s32[]{:T(128)}, /*index=5*/bf16[8,192,192]{2...) while((s32[]{:T(128)}, f32[768,192]{0,1:T(8,128)S(1)}, ...), condition=%wide.region_8.8_spmd.clone, body=%wide.region_7.7_spmd.clone.sunk | while | flops 56844292 | bytes 1672871 | solution.py:110
  352.2 9.1 %while.64 = (s32[]{:T(128)}, f32[768,192]{0,1:T(8,128)S(1)}, s32[]{:T(128)}, bf16[8,768,2240]{2,1,0:T(8,128)(2,1)}, s32[]{:T(128)}, /*index=5*/bf16[8,192,192]{2...) while((s32[]{:T(128)}, f32[768,192]{0,1:T(8,128)S(1)}, ...), condition=%wide.region_8.8_spmd.clone, body=%wide.region_7.7_spmd.clone.sunk | while | flops 56844292 | bytes 1672871 | solution.py:110
  370.5 9.1 %while.64 = (s32[]{:T(128)}, f32[768,192]{0,1:T(8,128)S(1)}, s32[]{:T(128)}, bf16[8,768,2240]{2,1,0:T(8,128)(2,1)}, s32[]{:T(128)}, /*index=5*/bf16[8,192,192]{2...) while((s32[]{:T(128)}, f32[768,192]{0,1:T(8,128)S(1)}, ...), condition=%wide.region_8.8_spmd.clone, body=%wide.region_7.7_spmd.clone.sunk | while | flops 56844292 | bytes 1672871 | solution.py:110
  388.8 9.1 %while.64 = (s32[]{:T(128)}, f32[768,192]{0,1:T(8,128)S(1)}, s32[]{:T(128)}, bf16[8,768,2240]{2,1,0:T(8,128)(2,1)}, s32[]{:T(128)}, /*index=5*/bf16[8,192,192]{2...) while((s32[]{:T(128)}, f32[768,192]{0,1:T(8,128)S(1)}, ...), condition=%wide.region_8.8_spmd.clone, body=%wide.region_7.7_spmd.clone.sunk | while | flops 56844292 | bytes 1672871 | solution.py:110
  407.1 9.1 %while.64 = (s32[]{:T(128)}, f32[768,192]{0,1:T(8,128)S(1)}, s32[]{:T(128)}, bf16[8,768,2240]{2,1,0:T(8,128)(2,1)}, s32[]{:T(128)}, /*index=5*/bf16[8,192,192]{2...) while((s32[]{:T(128)}, f32[768,192]{0,1:T(8,128)S(1)}, ...), condition=%wide.region_8.8_spmd.clone, body=%wide.region_7.7_spmd.clone.sunk | while | flops 56844292 | bytes 1672871 | solution.py:110
  425.3 9.1 %while.64 = (s32[]{:T(128)}, f32[768,192]{0,1:T(8,128)S(1)}, s32[]{:T(128)}, bf16[8,768,2240]{2,1,0:T(8,128)(2,1)}, s32[]{:T(128)}, /*index=5*/bf16[8,192,192]{2...) while((s32[]{:T(128)}, f32[768,192]{0,1:T(8,128)S(1)}, ...), condition=%wide.region_8.8_spmd.clone, body=%wide.region_7.7_spmd.clone.sunk | while | flops 56844292 | bytes 1672871 | solution.py:110
  443.6 9.1 %while.64 = (s32[]{:T(128)}, f32[768,192]{0,1:T(8,128)S(1)}, s32[]{:T(128)}, bf16[8,768,2240]{2,1,0:T(8,128)(2,1)}, s32[]{:T(128)}, /*index=5*/bf16[8,192,192]{2...) while((s32[]{:T(128)}, f32[768,192]{0,1:T(8,128)S(1)}, ...), condition=%wide.region_8.8_spmd.clone, body=%wide.region_7.7_spmd.clone.sunk | while | flops 56844292 | bytes 1672871 | solution.py:110
  456.9 5.8 slice.19
  462.7 6.6 copy.16
  472.1 245.3 %all-reduce.5.cloned.1.call-done = f32[4,192,2048]{2,1,0:T(8,128)} async-done(((f32[4,192,2048]{2,1,0:T(8,128)}), f32[4,192,2048]{2,1,0:T(8,128)}) %all-reduce.5.cloned.1.call-update) | async-done | bytes 6291472 | tf_op jit(solution)/shard_map/psum | solution.py:125
  717.4 4.7 fusion.49
  722.1 4.6 multiply_reduce_fusion
  726.7 9.3 %all_to_all.11 = f32[4,1,2]{2,1,0:T(1,128)S(1)} all-to-all(f32[4,1,2]{2,1,0:T(1,128)S(1)} %broadcast_in_dim.42), channel_id=1, replica_groups=mesh['ops'=32,'site'=4] {'site'}, dimensions={0} | all-to-all | bytes 64 | tf_op jit(solution)/shard_map/all_to_all | solution.py:9
  (225 shorter events, 246.6 us)
Async XLA Ops:
  15.4 6.6 copy-start.4
  15.4 15.0 %copy-start.5 = (s32[2048]{0:T(1024)S(1)}, s32[2048]{0:T(1024)}, u32[]{:S(2)}) copy-start(s32[2048]{0:T(1024)} %param.19) | copy-start | bytes 24580
  15.4 145.6 %all-to-all-start = ((bf16[4,8,4,192,192]{4,3,1,2,0:T(8,128)(2,1)}), bf16[4,8,4,192,192]{4,3,1,2,0:T(8,128)(2,1)}, u32[]{:S(2)}, u32[]{:S(2)}) async-start(bf16[4,8,4,192,192]{4,3,1,2,0:T(8,128)(2,1)} %stack.44), calls=%async_computation | async-start | bytes 25165824 | tf_op jit(solution)/shard_map/all_to_all | solution.py:89
  22.0 695.4 %all-reduce.5.cloned.1.call-start = ((), (), s32[]{:S(2)}) async-start(), calls=%async_computation.2 | async-start | bytes 12582912 | tf_op jit(solution)/shard_map/psum | solution.py:125
  469.3 2.7 copy-start.3
  469.3 248.1 %copy-start = (bf16[192,2048]{1,0:T(8,128)(2,1)S(1)}, bf16[192,2048]{1,0:T(8,128)(2,1)}, u32[]{:S(2)}) copy-start(bf16[192,2048]{1,0:T(8,128)(2,1)} %get-tuple-element.835) | copy-start | bytes 2359300
  469.3 248.1 %copy-start.1 = (bf16[192,2048]{1,0:T(8,128)(2,1)S(1)}, bf16[192,2048]{1,0:T(8,128)(2,1)}, u32[]{:S(2)}) copy-start(bf16[192,2048]{1,0:T(8,128)(2,1)} %get-tuple-element.836) | copy-start | bytes 2359300
  469.3 248.1 %copy-start.2 = (f32[2048]{0:T(1024)S(1)}, f32[2048]{0:T(1024)}, u32[]{:S(2)}) copy-start(f32[2048]{0:T(1024)} %param.22) | copy-start | bytes 24580
Sparse Core Ops, SparseCore 0:
  469.5 247.9 all-reduce.4
